TPU v7x, 32 devices: a whole 2x2x4 slice. The times are simulated.
32 devices in a mesh: seq: 8 (over z, y), head: 4 (over x, core).
Axes of the slice: x: 2, y: 2, z: 4, core: 2. Of those that a mesh axis runs over, the one named last changes fastest.
Arguments:
- cache: bfloat16 [1024, 576], P('seq'), may hold values from -8 to 8
- query_nope: bfloat16 [1024, 4096], P('seq', 'head'), may hold values from -5 to 5
- query_rope: bfloat16 [1024, 2048], P('seq', 'head'), may hold values from -256 to 256
- scale_exp: int32 [1024], P('seq'), may hold values from -1 to 1
- offsets: int32 [16], P('seq'), may hold values from 0 to 960
- up_key: bfloat16 [512, 4096], P(None, 'head'), may hold values from -0.25 to 0.25
- up_value: bfloat16 [512, 4096], P(None, 'head'), may hold values from -0.25 to 0.25
- grad_out: bfloat16 [1024, 4096], P('seq', 'head'), may hold values from -5 to 5
Outputs:
- d_cache: bfloat16 [1024, 576], P('seq')
- d_query_nope: bfloat16 [1024, 4096], P('seq', 'head')
- d_query_rope: bfloat16 [1024, 2048], P('seq', 'head')
All inputs are finite; a program needn't handle non-finite values.
Results may differ from a plain program's by a relative error of at most 0.0099.
Values may be sent and summed in bfloat16 or wider, within the bound.
A program may use at most 64 MiB of HBM per device.

v0:
```python
import math

import jax
import jax.numpy as jnp
from jax import lax
from jax.sharding import PartitionSpec as P

LATENT = 512
ROPE = 64
NOPE = 128
QBLOCK = 64


def per_device(cache, query_nope, query_rope, scale_exp, offsets, up_key, up_value, grad_out):
    width = cache.shape[1]
    own_keys = cache.shape[0]
    packed = cache.reshape(own_keys // 2, 2 * width)
    whole = lax.all_gather(packed, "seq", axis=0, tiled=True).reshape(-1, width)
    keys_total = whole.shape[0]
    queries = query_nope.shape[0]
    heads = up_key.shape[1] // NOPE
    scale = (NOPE + ROPE) ** (-0.5)
    factor = jnp.exp2(scale_exp.astype(jnp.float32))[:, None]
    q_nope = (
        (query_nope.astype(jnp.float32) * factor).astype(jnp.bfloat16).reshape(queries, heads, NOPE)
    )
    q_rope = (
        (query_rope.astype(jnp.float32) * factor).astype(jnp.bfloat16).reshape(queries, heads, ROPE)
    )
    w_key = up_key.reshape(LATENT, heads, NOPE)
    w_value = up_value.reshape(LATENT, heads, NOPE)
    absorbed = jnp.einsum("qhd,chd->hqc", q_nope, w_key, preferred_element_type=jnp.float32).astype(
        jnp.bfloat16
    )
    extended = jnp.concatenate([absorbed, jnp.transpose(q_rope, (1, 0, 2))], axis=2)
    back = jnp.einsum(
        "qhd,chd->hqc",
        grad_out.reshape(queries, heads, NOPE),
        w_value,
        preferred_element_type=jnp.float32,
    ).astype(jnp.bfloat16)
    positions = (offsets[:, None] + jnp.arange(QBLOCK, dtype=jnp.int32)[None, :]).reshape(-1)
    latent = whole[:, :LATENT]
    group = math.gcd(heads, max(1, 512 // queries))
    visible = (
        jnp.arange(keys_total, dtype=jnp.int32)[None, :] <= jnp.tile(positions, group)[:, None]
    )
    along_rows = (((0,), (0,)), ((), ()))
    along_cols = (((1,), (1,)), ((), ()))
    d_cache = jnp.zeros((keys_total, width), jnp.float32)
    nope_parts = []
    rope_parts = []
    for first in range(0, heads, group):
        ext_rows = extended[first : first + group].reshape(group * queries, width)
        back_rows = back[first : first + group].reshape(group * queries, LATENT)
        raw = (
            lax.dot_general(ext_rows, whole, along_cols, preferred_element_type=jnp.float32) * scale
        )
        scores = jnp.where(visible, raw, -jnp.inf)
        top = jnp.max(scores, axis=1, keepdims=True)
        lse = top + jnp.log(jnp.sum(jnp.exp(scores - top), axis=1, keepdims=True))
        probs = jnp.exp(scores - lse)
        probs_b = probs.astype(jnp.bfloat16)
        latent_out = jnp.dot(probs_b, latent, preferred_element_type=jnp.float32)
        delta = jnp.sum(back_rows.astype(jnp.float32) * latent_out, axis=1, keepdims=True)
        dprob = lax.dot_general(back_rows, latent, along_cols, preferred_element_type=jnp.float32)
        dscore = (probs * (dprob - delta) * scale).astype(jnp.bfloat16)
        grad_ext = jnp.dot(dscore, whole, preferred_element_type=jnp.float32)
        d_cache = d_cache + lax.dot_general(
            dscore, ext_rows, along_rows, preferred_element_type=jnp.float32
        )
        d_cache = d_cache.at[:, :LATENT].add(
            lax.dot_general(probs_b, back_rows, along_rows, preferred_element_type=jnp.float32)
        )
        grad_abs = grad_ext[:, :LATENT].astype(jnp.bfloat16).reshape(group, queries, LATENT)
        part_nope = (
            jnp.einsum(
                "hqc,chd->qhd",
                grad_abs,
                w_key[:, first : first + group],
                preferred_element_type=jnp.float32,
            )
            * factor[:, :, None]
        )
        part_rope = (
            jnp.transpose(grad_ext[:, LATENT:].reshape(group, queries, ROPE), (1, 0, 2))
            * factor[:, :, None]
        )
        nope_parts.append(part_nope.astype(jnp.bfloat16))
        rope_parts.append(part_rope.astype(jnp.bfloat16))
    d_query_nope = jnp.concatenate(nope_parts, axis=1).reshape(queries, heads * NOPE)
    d_query_rope = jnp.concatenate(rope_parts, axis=1).reshape(queries, heads * ROPE)
    seq_count = lax.axis_size("seq")
    head_count = lax.axis_size("head")
    shares = lax.psum_scatter(
        d_cache.reshape(seq_count * head_count, -1),
        ("seq", "head"),
        scatter_dimension=0,
        tiled=True,
    )
    mine = lax.all_gather(shares, "head", axis=0, tiled=True).reshape(-1, width)
    return (mine.astype(jnp.bfloat16), d_query_nope, d_query_rope)


def solution(mesh):
    in_specs = (
        P("seq", None),
        P("seq", "head"),
        P("seq", "head"),
        P("seq"),
        P("seq"),
        P(None, "head"),
        P(None, "head"),
        P("seq", "head"),
    )
    out_specs = (P("seq", None), P("seq", "head"), P("seq", "head"))
    return jax.shard_map(
        per_device, mesh=mesh, in_specs=in_specs, out_specs=out_specs, check_vma=False
    )
```

profile of v0, /device:TPU:0, one launch (start us, length us, event | category | flops | bytes accessed | tf_op | source)
XLA Modules:
  0.0 168.9 jit_solution(14242522594931974247)
XLA Ops:
  7.2 0.0 copy-start
  7.2 0.0 copy-start.9
  7.2 0.0 all-gather.3.cloned.1.call-start
  7.3 1.2 copy.45
  8.5 0.8 reshape.153
  9.3 0.0 all-gather.3.cloned.1.call-update
  9.3 1.0 copy.43
  10.4 0.7 multiply_exponential_fusion
  11.1 0.9 copy.44
  11.9 0.5 copy.40
  12.5 0.0 copy-done.15
  12.5 0.0 copy-start.3
  12.5 0.1 iota_add_fusion
  12.6 0.1 add.58
  12.6 0.4 convolution_convert_fusion
  13.1 0.0 copy-start.14
  13.1 0.1 fusion.32
  13.2 0.0 copy-start.1
  13.2 1.0 copy.48
  14.2 1.0 copy.49
  15.2 0.7 compare_reduce_fusion
  15.9 0.5 convolution_convert_fusion.1
  16.4 1.1 pad_maximum_fusion
  17.5 37.2 %all-gather.3.cloned.1.call-done = bf16[512,1152]{1,0:T(8,128)(2,1)} async-done(((bf16[64,1152]{1,0:T(8,128)(2,1)}), bf16[512,1152]{1,0:T(8,128)(2,1)}) %all-gather.3.cloned.1.call-update) | async-done | bytes 1179664 | tf_op jit(solution)/shard_map/all_gather | solution.py:18
  54.7 3.4 %reshape.154 = bf16[1024,576]{1,0:T(8,128)(2,1)} reshape(bf16[512,1152]{1,0:T(8,128)(2,1)} %all-gather.3.cloned.1.call-done) | data formatting | bytes 2359296 | tf_op jit(solution)/shard_map/reshape | solution.py:18
  58.1 2.5 %fusion.33 = (f32[512]{0:T(512)S(1)}, f32[512,1024]{1,0:T(8,128)S(1)}) fusion(bf16[512,576]{1,0:T(8,128)(2,1)S(1)} %bitcast.90, bf16[1024,576]{1,0:T(8,128)(2,1)} %reshape.154, s32[512]{0:T(512)S(1)} %broadcast_bitcast_fusion), kind=kOutput, calls=%fused_computation.68 | convolution fusion | flops 606076416 | bytes 3870720 | tf_op jit(solution)/shard_map/dot_general | solution.py:57
  60.6 0.0 copy-start.11
  60.6 0.5 exponential_reduce_fusion.1
  61.1 0.8 copy-done.8
  61.9 0.1 copy-done.11
  62.0 0.9 fusion.4
  62.9 0.8 multiply_convert_fusion.1
  63.7 0.8 fusion.35
  64.5 0.8 fusion.36
  65.4 0.0 copy-done.5
  65.4 1.2 fusion.34
  66.6 0.5 exponential_reduce_fusion
  67.1 0.5 copy-done.10
  67.6 0.9 fusion.5
  68.5 0.8 multiply_convert_fusion
  69.3 0.8 fusion.37
  70.1 0.9 slice.123
  71.0 0.9 slice.124
  71.9 0.7 slice_bitcast_fusion
  72.5 1.9 %fusion = f32[1024,576]{0,1:T(8,128)S(1)} fusion(f32[1024,576]{0,1:T(8,128)S(1)} %fusion.35, bf16[512,512]{1,0:T(8,128)(2,1)S(1)} %bitcast.84, pred[]{:T(512)} %compare_reduce_fusion, f32[512,1024]{1,0:T(8,128)S(1)} %get-tuple-element.43, f32[512]{0:T(512)S(1)} %log_add_fusion.1), kind=kOutput, calls=%fused_computation.2 | convolution fusion | flops 538968064 | bytes 6817793 | tf_op jit(solution)/shard_map/dot_general | solution.py:73
  74.4 0.9 convolution_add_fusion
  75.3 0.2 copy-done.2
  75.5 1.8 %fusion.1 = f32[1024,576]{0,1:T(8,128)S(1)} fusion(f32[1024,576]{0,1:T(8,128)S(1)} %convolution_add_fusion, bf16[512,512]{1,0:T(8,128)(2,1)S(1)} %bitcast.81, pred[]{:T(512)} %compare_reduce_fusion, f32[512,1024]{1,0:T(8,128)S(1)} %get-tuple-element.45, f32[512]{0:T(512)S(1)} %log_add_fusion), kind=kOutput, calls=%fused_computation.3 | convolution fusion | flops 538968064 | bytes 6817793 | tf_op jit(solution)/shard_map/dot_general | solution.py:73
  77.3 2.1 %copy.50 = f32[1024,576]{1,0:T(8,128)} copy(f32[1024,576]{0,1:T(8,128)S(1)} %fusion.1) | data formatting | bytes 4718592 | tf_op jit(solution)/shard_map/scatter-add | solution.py:72
  79.4 2.5 %reshape.160 = f32[32,18432]{1,0:T(8,128)S(1)} reshape(f32[1024,576]{1,0:T(8,128)} %copy.50) | data formatting | bytes 4718592 | tf_op jit(solution)/shard_map/reshape | solution.py:96
  81.9 67.4 %all-reduce.2 = bf16[32,18432]{1,0:T(8,128)(2,1)} all-reduce(f32[32,18432]{1,0:T(8,128)S(1)} %reshape.160), channel_id=2, replica_groups=mesh['seq'=8,'head'=4] {'seq','head'}, use_global_device_ids=true, to_apply=%region_7.8.clone | all-reduce | flops 589824 | bytes 3538944
  149.3 1.2 dynamic-slice_bitcast_fusion
  150.5 5.9 %all-gather = bf16[4,1,18432]{2,1,0:T(2,128)(2,1)S(1)} all-gather(bf16[1,1,18432]{2,1,0:T(2,128)(2,1)S(1)} %dynamic-slice_bitcast_fusion), channel_id=1, replica_groups=mesh['seq'=8,'head'=4] {'head'}, dimensions={0}, use_global_device_ids=true | all-gather | bytes 184320 | tf_op jit(solution)/shard_map/all_gather | solution.py:101
  156.4 0.9 convert_reduce_fusion
  157.2 0.2 convert_element_type.85
  157.4 0.8 copy.55
  158.2 1.3 copy.60
  159.5 0.0 copy-start.12
  159.5 0.3 fusion.8
  159.8 0.0 copy-done.7
  159.8 0.2 copy.59
  160.0 0.3 fusion.9
  160.4 0.9 copy.56
  161.3 0.8 copy.57
  (25 shorter events, 0.2 us)
Async XLA Ops:
  7.2 5.5 %copy-start = (bf16[512,1024]{1,0:T(8,128)(2,1)S(1)}, bf16[512,1024]{1,0:T(8,128)(2,1)}, u32[]{:S(2)}) copy-start(bf16[512,1024]{1,0:T(8,128)(2,1)} %param.18) | copy-start | bytes 3145732
  7.2 4.7 %copy-start.9 = (bf16[512,1024]{1,0:T(8,128)(2,1)S(1)}, bf16[512,1024]{1,0:T(8,128)(2,1)}, u32[]{:S(2)}) copy-start(bf16[512,1024]{1,0:T(8,128)(2,1)} %param.17) | copy-start | bytes 3145732
  7.2 5.3 %copy-start.15 = (s32[2]{0:T(128)S(1)}, s32[2]{0:T(128)}, u32[]{:S(2)}) copy-start(s32[2]{0:T(128)} %param.16) | copy-start | bytes 28
  7.2 5.4 %copy-start.13 = (bf16[128,1024]{1,0:T(8,128)(2,1)S(1)}, bf16[128,1024]{1,0:T(8,128)(2,1)}, u32[]{:S(2)}) copy-start(bf16[128,1024]{1,0:T(8,128)(2,1)} %param.19) | copy-start | bytes 786436
  7.2 47.4 %all-gather.3.cloned.1.call-start = ((), (), s32[]{:S(2)}) async-start(), calls=%async_computation | async-start | bytes 1327104 | tf_op jit(solution)/shard_map/all_gather | solution.py:18
  12.5 3.4 %copy-start.3 = (bf16[512,1024]{0,1:T(8,128)(2,1)}, bf16[512,1024]{0,1:T(8,128)(2,1)S(1)}, u32[]{:S(2)}) copy-start(bf16[512,1024]{0,1:T(8,128)(2,1)S(1)} %copy.40) | copy-start | bytes 3145732
  13.1 2.8 %copy-start.14 = (bf16[128,1024]{1,0:T(8,128)(2,1)S(1)}, bf16[128,1024]{1,0:T(8,128)(2,1)}, u32[]{:S(2)}) copy-start(bf16[128,1024]{1,0:T(8,128)(2,1)} %param.13) | copy-start | bytes 786436
  13.2 55.3 %copy-start.1 = (bf16[4,128,512]{2,1,0:T(8,128)(2,1)}, bf16[4,128,512]{2,1,0:T(8,128)(2,1)S(1)}, u32[]{:S(2)}) copy-start(bf16[4,128,512]{2,1,0:T(8,128)(2,1)S(1)} %get-tuple-element.38) | copy-start | bytes 1572868
  17.5 47.9 %copy-start.5 = (bf16[4,128,576]{2,1,0:T(8,128)(2,1)}, bf16[4,128,576]{2,1,0:T(8,128)(2,1)S(1)}, u32[]{:S(2)}) copy-start(bf16[4,128,576]{2,1,0:T(8,128)(2,1)S(1)} %get-tuple-element.36) | copy-start | bytes 1769476
  60.6 1.3 copy-start.8
  60.6 1.4 copy-start.11
  66.5 1.0 copy-start.10
  72.5 1.9 %copy-start.6 = (bf16[4,128,576]{2,1,0:T(8,128)(2,1)S(1)}, bf16[4,128,576]{2,1,0:T(8,128)(2,1)}, u32[]{:S(2)}) copy-start(bf16[4,128,576]{2,1,0:T(8,128)(2,1)} %copy-done.5) | copy-start | bytes 1769476
  74.4 1.0 copy-start.2
  149.3 10.2 %copy-start.4 = (bf16[512,1024]{0,1:T(8,128)(2,1)S(1)}, bf16[512,1024]{0,1:T(8,128)(2,1)}, u32[]{:S(2)}) copy-start(bf16[512,1024]{0,1:T(8,128)(2,1)} %copy-done.3) | copy-start | bytes 3145732
  149.3 10.5 %copy-start.7 = (bf16[512,512]{0,1:T(8,128)(2,1)S(1)}, bf16[512,512]{0,1:T(8,128)(2,1)}, u32[]{:S(2)}) copy-start(bf16[512,512]{0,1:T(8,128)(2,1)} %slice.124) | copy-start | bytes 1572868
  159.5 1.7 %copy-start.12 = (f32[8,4,8,128]{3,2,1,0:T(8,128)S(1)}, f32[8,4,8,128]{3,2,1,0:T(8,128)}, u32[]{:S(2)}) copy-start(f32[8,4,8,128]{3,2,1,0:T(8,128)} %get-tuple-element.47) | copy-start | bytes 393220
Sparse Core Ops, SparseCore 0:
  10.8 43.8 all-gather.2
where the time goes:
time: 169 us
  blocking collectives  73.3 us (43%)
  waiting for transfers between devices  37.2 us (22%)
  local copies, waits for them, and re-layouts  24.9 us (15%)
  matrix products  15.5 us (9%)
  between operations  14.4 us (9%)
  other arithmetic  3.61 us (2%)
    unnamed x1, blocking collectives  67.4 us
    all_gather x1, waiting for transfers between devices, per_device(): whole = lax.all_gather(packed, 'seq', axis=0, tiled=True).reshape(-1, width)  37.2 us
    unnamed x40, local copies, waits for them, and re-layouts  8.68 us
    all_gather x1, blocking collectives, per_device(): mine = lax.all_gather(shares, 'head', axis=0, tiled=True).reshape(-1, width)  5.87 us
    dot_general x2, matrix products, per_device(): lax.dot_general(probs_b, back_rows, along_rows, preferred_element_type=jn...  3.67 us
    dot_general x2, matrix products, per_device(): lax.dot_general(ext_rows, whole, along_cols, preferred_element_type=jnp.f...  3.64 us
    reshape x1, local copies, waits for them, and re-layouts, per_device(): whole = lax.all_gather(packed, 'seq', axis=0, tiled=True).reshape(-1, width)  3.44 us
  transfers between devices with their start and end apart: 1, of which 1 were waited for; matrix products, arithmetic and copies ran while one was open for 5% of the time, Pallas kernels for 0%

commit v1 on v0

v1 whole, which is shorter than its diff:
```python
import functools
import math

import jax
import jax.numpy as jnp
from jax import lax
from jax.experimental import pallas as pl
from jax.experimental.pallas import tpu as pltpu
from jax.sharding import PartitionSpec as P

LATENT = 512
ROPE = 64
NOPE = 128
QBLOCK = 64
MESH = pl.DeviceIdType.MESH
BF16 = jnp.bfloat16
F32 = jnp.float32
NEG = -1e30


def dot(a, b):
    return jnp.dot(a, b, preferred_element_type=F32)


def dot_nt(a, b):
    return lax.dot_general(a, b, (((1,), (1,)), ((), ())), preferred_element_type=F32)


def kernel(
    nz, nx,
    cache_ref, qn_ref, qr_ref, se_ref, off_ref, uk_ref, uv_ref, go_ref,
    dc_ref, dqn_ref, dqr_ref,
    full, cT, extT, ext, backT, back, upkT, S, dP, pT, dsT, mx, D,
    csnd, crcv, ysnd, yrcv, zsnd, zrcv, xsnd, xrcv, fin, rfin,
    gz_send, gy_send, gc_send, g_recv,
    c_send, c_recv, y_send, y_recv, z_send, z_recv, x_send, x_recv, f_send, f_recv,
):
    own, width = cache_ref.shape
    half = own // 2
    pair = 2 * own
    queries = qn_ref.shape[0]
    heads = qn_ref.shape[1] // NOPE
    rows = heads * queries
    scale = (NOPE + ROPE) ** (-0.5)
    s_me = lax.axis_index("seq")
    h_me = lax.axis_index("head")
    z, y = s_me // 2, lax.rem(s_me, 2)
    x, core = h_me // 2, lax.rem(h_me, 2)
    oy, oc = 1 - y, 1 - core

    def z_dev(zz):
        return (zz * 2 + y, h_me)

    y_dev = (z * 2 + oy, h_me)
    c_dev = (s_me, x * 2 + oc)

    def x_dev(xx):
        return (s_me, xx * 2 + core)

    zs = [lax.rem(z + k, nz) for k in range(nz)]
    xs = [lax.rem(x + k, nx) for k in range(nx)]

    barrier = pltpu.get_barrier_semaphore()
    peers = [z_dev(zz) for zz in zs[1:]] + [y_dev, c_dev] + [x_dev(xx) for xx in xs[1:]]
    for dev in peers:
        pl.semaphore_signal(barrier, inc=1, device_id=dev, device_id_type=MESH)
    pl.semaphore_wait(barrier, len(peers))

    def remote(src, dst, send, recv, dev):
        return pltpu.make_async_remote_copy(
            src_ref=src, dst_ref=dst, send_sem=send, recv_sem=recv,
            device_id=dev, device_id_type=MESH,
        )

    def half_rows(blk, hf):
        return pl.ds(pl.multiple_of(blk * own + hf * half, half), half)

    def gather(src, blk, hf, send, dev):
        return remote(src, full.at[half_rows(blk, hf)], send, g_recv.at[blk * 2 + hf], dev)

    sends = []
    mine = cache_ref.at[pl.ds(pl.multiple_of(core * half, half), half)]

    def go(copy):
        copy.start()
        sends.append(copy)

    go(gather(mine, s_me, core, gy_send.at[0], y_dev))
    for k in range(1, nz):
        go(gather(mine, s_me, core, gz_send.at[k], z_dev(zs[k])))

    full[pl.ds(pl.multiple_of(s_me * own, own), own), :] = cache_ref[...]
    factor = jnp.exp2(se_ref[...].astype(F32))
    lane = lax.broadcasted_iota(jnp.int32, (1, queries), 1)
    pos = jnp.zeros((1, queries), jnp.int32)
    for b in range(queries // QBLOCK):
        inside = (lane >= b * QBLOCK) & (lane < (b + 1) * QBLOCK)
        pos = jnp.where(inside, off_ref[b] + lane - b * QBLOCK, pos)

    for h in range(heads):
        cols = slice(h * NOPE, (h + 1) * NOPE)
        qs = slice(h * queries, (h + 1) * queries)
        w = uk_ref[:, cols]
        a = (dot_nt(w, qn_ref[:, cols]) * factor).astype(BF16)
        extT[0:LATENT, qs] = a
        ext[qs, 0:LATENT] = a.T
        upkT[cols, :] = w.T
        g = dot_nt(uv_ref[:, cols], go_ref[:, cols]).astype(BF16)
        backT[:, qs] = g
        back[qs, :] = g.T
    for h in range(0, heads, 2):
        r = (qr_ref[:, h * ROPE : (h + 2) * ROPE].astype(F32).T * factor).astype(BF16)
        for i in range(2):
            part = r[i * ROPE : (i + 1) * ROPE, :]
            qs = slice((h + i) * queries, (h + i + 1) * queries)
            extT[LATENT:width, qs] = part
            ext[qs, LATENT:width] = part.astype(F32).T.astype(BF16)
    mx[...] = jnp.full(mx.shape, NEG, F32)

    tile = 2 * queries
    pos2 = jnp.concatenate([pos, pos], axis=1)

    def scores(zz):
        base = pl.multiple_of(zz * pair, pair)
        c = full[pl.ds(base, pair), :]
        key = base + lax.broadcasted_iota(jnp.int32, (pair, tile), 0)
        seen = key <= pos2
        for t in range(rows // tile):
            ls = slice(t * tile, (t + 1) * tile)
            s = dot(c, extT[:, ls]) * (scale * math.log2(math.e))
            s = jnp.where(seen, s, NEG)
            S[pl.ds(base, pair), ls] = s
            mx[:, ls] = jnp.maximum(mx[:, ls], jnp.max(s.reshape(pair // 8, 8, tile), axis=0))
            dP[pl.ds(base, pair), ls] = dot(c[:, :LATENT], backT[:, ls])
        cT[:, pl.ds(base, pair)] = c.T

    def got(blk, hf):
        gather(mine, blk, hf, gy_send.at[0], c_dev).wait_recv()

    def forward(blk, send, dev):
        go(gather(full.at[half_rows(blk, core)], blk, core, send, dev))

    for k in range(nz + 2):
        if 1 <= k < nz:
            blk = zs[k] * 2 + y
            got(blk, core)
            forward(blk, gy_send.at[k], y_dev)
            forward(blk, gc_send.at[k], c_dev)
        if 1 <= k <= nz:
            blk = zs[k - 1] * 2 + oy
            got(blk, core)
            forward(blk, gc_send.at[nz + k - 1], c_dev)
        if k >= 2:
            zz = zs[k - 2]
            if k > 2:
                got(zz * 2 + y, oc)
            got(zz * 2 + oy, oc)
            scores(zz)

    keys = full.shape[0]
    chunk = own

    def soften(h, carry):
        ls = pl.ds(pl.multiple_of(h * queries, queries), queries)
        top = jnp.max(mx[:, ls], axis=0, keepdims=True)
        tot = jnp.zeros((8, queries), F32)
        dl = jnp.zeros((8, queries), F32)
        for i in range(keys // chunk):
            rs = slice(i * chunk, (i + 1) * chunk)
            p = jnp.exp2(S[rs, ls] - top)
            S[rs, ls] = p
            tot = tot + jnp.sum(p.reshape(chunk // 8, 8, queries), axis=0)
            dl = dl + jnp.sum((p * dP[rs, ls]).reshape(chunk // 8, 8, queries), axis=0)
        inv = 1.0 / jnp.sum(tot, axis=0, keepdims=True)
        delta = jnp.sum(dl, axis=0, keepdims=True) * inv
        for i in range(keys // chunk):
            rs = slice(i * chunk, (i + 1) * chunk)
            pr = S[rs, ls] * inv
            pT[rs, ls] = pr.astype(BF16)
            dsT[rs, ls] = (pr * (dP[rs, ls] - delta) * scale).astype(BF16)
        return carry

    lax.fori_loop(0, heads, soften, 0)

    def core_copy(zz, i):
        return remote(csnd.at[zz], crcv.at[zz], c_send.at[zz], c_recv.at[zz], c_dev)

    def y_copy(zz):
        return remote(ysnd.at[zz], yrcv.at[zz], y_send.at[zz], y_recv.at[zz], y_dev)

    def step_d(k):
        zz = zs[k]
        rs = pl.ds(pl.multiple_of(zz * pair, pair), pair)
        ds, pb = dsT[rs, :], pT[rs, :]
        D[rs, 0:LATENT] = dot(ds, ext[:, 0:LATENT]) + dot(pb, back[...])
        D[rs, LATENT:width] = dot(ds, ext[:, LATENT:width])
        for yy in range(2):
            csnd[zz, yy] = D[half_rows(zz * 2 + yy, oc), :].astype(BF16)
        go(core_copy(zz, 0))

    def step_e(k):
        zz = zs[k]
        core_copy(zz, 0).wait_recv()
        t = D[half_rows(zz * 2 + oy, core), :] + crcv[zz, oy].astype(F32)
        ysnd[zz] = t.astype(BF16)
        go(y_copy(zz))

    def step_f(k):
        zz = zs[k]
        y_copy(zz).wait_recv()
        u = (
            D[half_rows(zz * 2 + y, core), :]
            + crcv[zz, y].astype(F32)
            + yrcv[zz].astype(F32)
        )
        if k:
            zsnd[zz] = u.astype(BF16)
            go(remote(zsnd.at[zz], zrcv.at[z], z_send.at[zz], z_recv.at[z], z_dev(zz)))
        return u

    def grads(h):
        g = dot(cT[...], dsT[:, h * queries : (h + 2) * queries])
        lo = g[0:LATENT].astype(BF16)
        hi = g[LATENT:width]
        ropes = []
        for i in range(2):
            qs = slice(i * queries, (i + 1) * queries)
            cols = slice((h + i) * NOPE, (h + i + 1) * NOPE)
            d = dot(upkT[cols, :], lo[:, qs]) * factor
            dqn_ref[:, cols] = d.T.astype(BF16)
            ropes.append(hi[:, qs] * factor)
        dqr_ref[:, h * ROPE : (h + 2) * ROPE] = jnp.concatenate(ropes, axis=0).T.astype(BF16)

    order = list(range(1, nz)) + [0]
    pieces = list(range(0, heads, 2))
    for i, k in enumerate(order):
        step_d(k)
        if i:
            step_e(order[i - 1])
    grads(pieces.pop(0))
    step_e(order[-1])
    for k in order[:-1]:
        step_f(k)
        if pieces:
            grads(pieces.pop(0))
    while pieces:
        grads(pieces.pop(0))
    v = step_f(0)
    for k in range(1, nz):
        remote(
            zsnd.at[zs[k]], zrcv.at[zs[k]], z_send.at[zs[k]], z_recv.at[zs[k]], z_dev(zs[k])
        ).wait_recv()
        v = v + zrcv[zs[k]].astype(F32)
    vb = v.astype(BF16)
    xsnd[...] = vb
    for k in range(1, nx):
        go(remote(xsnd, xrcv.at[x], x_send.at[xs[k]], x_recv.at[x], x_dev(xs[k])))
    xrcv[x] = vb
    for k in range(1, nx):
        remote(
            xsnd, xrcv.at[xs[k]], x_send.at[xs[k]], x_recv.at[xs[k]], x_dev(xs[k])
        ).wait_recv()
    w = xrcv[0].astype(F32)
    for i in range(1, nx):
        w = w + xrcv[i].astype(F32)
    wb = w.astype(BF16)
    fin[...] = wb
    last = remote(fin, rfin, f_send.at[0], f_recv.at[0], c_dev)
    go(last)
    dc_ref[pl.ds(pl.multiple_of(core * half, half), half), :] = wb
    last.wait_recv()
    dc_ref[pl.ds(pl.multiple_of(oc * half, half), half), :] = rfin[...]
    for copy in sends:
        copy.wait_send()


def solution(mesh):
    seq, head = mesh.shape["seq"], mesh.shape["head"]
    nz, nx = seq // 2, head // 2

    def per_device(cache, qn, qr, se, off, uk, uv, go):
        own, width = cache.shape
        half = own // 2
        keys = own * seq
        queries = qn.shape[0]
        heads = qn.shape[1] // NOPE
        rows = heads * queries
        vm = pltpu.VMEM
        dma = pltpu.SemaphoreType.DMA
        vspec = pl.BlockSpec(memory_space=pltpu.VMEM)
        sspec = pl.BlockSpec(memory_space=pltpu.SMEM)
        return pl.pallas_call(
            functools.partial(kernel, nz, nx),
            out_shape=(
                jax.ShapeDtypeStruct(cache.shape, BF16),
                jax.ShapeDtypeStruct(qn.shape, BF16),
                jax.ShapeDtypeStruct(qr.shape, BF16),
            ),
            in_specs=[vspec, vspec, vspec, vspec, sspec, vspec, vspec, vspec],
            out_specs=(vspec, vspec, vspec),
            scratch_shapes=[
                vm((keys, width), BF16), vm((width, keys), BF16),
                vm((width, rows), BF16), vm((rows, width), BF16),
                vm((LATENT, rows), BF16), vm((rows, LATENT), BF16),
                vm((heads * NOPE, LATENT), BF16),
                vm((keys, rows), F32), vm((keys, rows), F32),
                vm((keys, rows), BF16), vm((keys, rows), BF16),
                vm((8, rows), F32), vm((keys, width), F32),
                vm((nz, 2, half, width), BF16), vm((nz, 2, half, width), BF16),
                vm((nz, half, width), BF16), vm((nz, half, width), BF16),
                vm((nz, half, width), BF16), vm((nz, half, width), BF16),
                vm((half, width), BF16), vm((nx, half, width), BF16),
                vm((half, width), BF16), vm((half, width), BF16),
                dma((nz,)), dma((nz,)), dma((2 * nz,)), dma((2 * seq,)),
                dma((nz,)), dma((nz,)), dma((nz,)), dma((nz,)),
                dma((nz,)), dma((nz,)), dma((nx,)), dma((nx,)), dma((1,)), dma((1,)),
            ],
            compiler_params=pltpu.CompilerParams(
                collective_id=0, has_side_effects=True, vmem_limit_bytes=60 * 1024 * 1024
            ),
        )(cache, qn, qr, se.reshape(1, -1), off, uk, uv, go)

    in_specs = (
        P("seq", None), P("seq", "head"), P("seq", "head"), P("seq"), P("seq"),
        P(None, "head"), P(None, "head"), P("seq", "head"),
    )
    out_specs = (P("seq", None), P("seq", "head"), P("seq", "head"))
    return jax.shard_map(
        per_device, mesh=mesh, in_specs=in_specs, out_specs=out_specs, check_vma=False
    )
```

time: 169 us -> 54.5 us (0.32)
  blocking collectives: 73.3 us -> 0 us
  Pallas kernels: 0 us -> 48.5 us
  waiting for transfers between devices: 37.2 us -> 0 us
  local copies, waits for them, and re-layouts: 24.9 us -> 5.11 us
  matrix products: 15.5 us -> 0 us
  between operations: 14.4 us -> 0.65 us
  other arithmetic: 3.61 us -> 0 us
    unnamed x1 -> x0, blocking collectives: 67.4 us -> none
    pallas_call x0 -> x1, Pallas kernels: none -> 48.5 us  [per_device(): pl.pallas_call(functools.partial(kernel, nz, nx), out_shape=(jax.ShapeDty...]
    all_gather x1 -> x0, waiting for transfers between devices: 37.2 us -> none  [per_device(): whole = lax.all_gather(packed, 'seq', axis=0, tiled=True).reshape(-1, width)]
    dot_general x16 -> x0, matrix products: 15.5 us -> none  [the longest x2 3.67 us: per_device(): lax.dot_general(probs_b, back_rows, along_rows, preferred_element_type=jn...]
    reshape x8 -> x0, local copies, waits for them, and re-layouts: 11.1 us -> none  [the longest x1 3.44 us: per_device(): whole = lax.all_gather(packed, 'seq', axis=0, tiled=True).reshape(-1, width)]
    all_gather x1 -> x0, blocking collectives: 5.87 us -> none  [per_device(): mine = lax.all_gather(shares, 'head', axis=0, tiled=True).reshape(-1, width)]
    unnamed x40 -> x7, local copies, waits for them, and re-layouts: 8.68 us -> 3.37 us
    scatter-add x1 -> x0, local copies, waits for them, and re-layouts: 2.11 us -> none  [per_device(): d_cache.at[:, :LATENT]]
  transfers between devices with their start and end apart: 1 -> 0, of which waited for: 1 -> 0; matrix products, arithmetic and copies ran while one was open for 5% -> 0% of each run, Pallas kernels for 0% -> 0%
where the time goes in v1:
time: 54.5 us; the launch traced here: 54.3 us
  Pallas kernels  48.5 us (89%)
  local copies, waits for them, and re-layouts  5.11 us (9%)
  between operations  0.65 us (1%)
    pallas_call x1, Pallas kernels, per_device(): pl.pallas_call(functools.partial(kernel, nz, nx), out_shape=(jax.ShapeDty...  48.5 us
    unnamed x7, local copies, waits for them, and re-layouts  3.37 us
    pallas_call x1, local copies, waits for them, and re-layouts, per_device(): pl.pallas_call(functools.partial(kernel, nz, nx), out_shape=(jax.ShapeDty...  1.74 us

profile of v1, /device:TPU:0, one launch (start us, length us, event | category | flops | bytes accessed | tf_op | source)
XLA Modules:
  0.0 54.3 jit_solution(7340278488112406580)
XLA Ops:
  0.6 1.7 %copy.11.cache_ref = bf16[128,576]{1,0:T(8,128)(2,1)} copy(bf16[128,576]{0,1:T(8,128)(2,1)} %param.8) | data formatting | bytes 294912 | tf_op args[0]
  2.3 48.5 %shard_map.103 = (bf16[128,576]{1,0:T(8,128)(2,1)}, bf16[128,1024]{1,0:T(8,128)(2,1)}, bf16[128,512]{1,0:T(8,128)(2,1)}) custom-call(bf16[128,576]{1,0:T(8,128)(2,1)} %copy.11.cache_ref, bf16[128,1024]{1,0:T(8,128)(2,1)} %qn_ref.1, bf16[128,512]{1,0:T(8,128)(2,1)} %qr_ref.1, s32[1,128]{1,0:T(1,128)} %bitcast.1, s32[2]{0:T(128)} %off_ref.1, ...), custom_call_target="tpu_custom_call" | custom-call | tf_op jit(solution)/shard_map/pallas_call | solution.py:292
  50.9 0.0 copy-start
  50.9 1.7 %copy.12 = bf16[128,576]{0,1:T(8,128)(2,1)} copy(bf16[128,576]{1,0:T(8,128)(2,1)} %get-tuple-element.3) | data formatting | bytes 294912 | tf_op jit(solution)/shard_map/pallas_call | solution.py:292
  52.6 0.0 copy-done
  52.7 0.0 copy-start.1
  52.7 0.7 %copy.15 = bf16[128,1024]{1,0:T(8,128)(2,1)} copy(bf16[128,1024]{1,0:T(8,128)(2,1)S(1)} %copy-done) | data formatting | bytes 524288
  53.4 0.3 copy-done.1
  53.7 0.7 %copy.16 = bf16[128,512]{1,0:T(8,128)(2,1)} copy(bf16[128,512]{1,0:T(8,128)(2,1)S(1)} %copy-done.1) | data formatting | bytes 262144
Async XLA Ops:
  50.9 1.8 %copy-start = (bf16[128,1024]{1,0:T(8,128)(2,1)S(1)}, bf16[128,1024]{1,0:T(8,128)(2,1)}, u32[]{:S(2)}) copy-start(bf16[128,1024]{1,0:T(8,128)(2,1)} %get-tuple-element.10) | copy-start | bytes 786436
  52.7 1.0 %copy-start.1 = (bf16[128,512]{1,0:T(8,128)(2,1)S(1)}, bf16[128,512]{1,0:T(8,128)(2,1)}, u32[]{:S(2)}) copy-start(bf16[128,512]{1,0:T(8,128)(2,1)} %get-tuple-element.11) | copy-start | bytes 393220
